TPU v7x, 32 devices: a whole 2x2x4 slice. The times are simulated.
32 devices in a mesh: var: 4 (over z), lat: 4 (over x, core), lon: 2 (over y).
Axes of the slice: x: 2, y: 2, z: 4, core: 2. Of those that a mesh axis runs over, the one named last changes fastest.
Arguments:
- state: bfloat16 [1, 256, 384, 1024], P(None, 'var', 'lat', 'lon'), may hold values from -6 to 6
- weights_in: bfloat16 [2, 256, 256], replicated, may hold values from -0.25 to 0.25
- bias_in: float32 [2, 256], replicated, may hold values from -3 to 3
- weights_out: bfloat16 [2, 256, 256], replicated, may hold values from -2 to 2
Outputs:
- field: bfloat16 [1, 256, 384, 1024], P(None, 'var', 'lat', 'lon')
- zonal: float32 [1, 256, 384], P(None, 'var', 'lat')
- energy: float32 [256], P('var')
All inputs are finite; a program needn't handle non-finite values.
Results may differ from a plain program's by a relative error of at most 0.012.
Values may be sent and summed in bfloat16 or wider, within the bound.
A program may use at most 64 MiB of HBM per device.

v0:
```python
import math
import jax
import jax.numpy as jnp
from jax import lax
from jax.sharding import PartitionSpec as P

LAT = 384
LON = 1024
MLAT = 96
MLON = 96


def lon_forward(first, count):
    index = first + jnp.arange(count, dtype=jnp.int32)
    modes = jnp.arange(MLON, dtype=jnp.int32)
    phase = index[:, None] * modes[None, :] % LON
    angle = phase.astype(jnp.float32) * (2.0 * math.pi / LON)
    scale = 1.0 / math.sqrt(LAT * LON)
    return (jnp.stack([jnp.cos(angle), -jnp.sin(angle)], 1) * scale).astype(jnp.bfloat16)


def lat_forward(first, count):
    freqs = jnp.arange(MLAT, dtype=jnp.int32) - MLAT // 2
    index = first + jnp.arange(count, dtype=jnp.int32)
    phase = jnp.mod(freqs[:, None] * index[None, :], LAT)
    angle = phase.astype(jnp.float32) * (2.0 * math.pi / LAT)
    cosine, sine = (jnp.cos(angle), jnp.sin(angle))
    return jnp.stack([jnp.stack([cosine, sine]), jnp.stack([-sine, cosine])])


def lat_inverse(first, count):
    freqs = jnp.arange(MLAT, dtype=jnp.int32) - MLAT // 2
    index = first + jnp.arange(count, dtype=jnp.int32)
    phase = jnp.mod(index[:, None] * freqs[None, :], LAT)
    angle = phase.astype(jnp.float32) * (2.0 * math.pi / LAT)
    cosine, sine = (jnp.cos(angle), jnp.sin(angle))
    return jnp.stack([jnp.stack([cosine, -sine]), jnp.stack([sine, cosine])]).astype(jnp.bfloat16)


def lon_inverse(first, count):
    modes = jnp.arange(MLON, dtype=jnp.int32)
    index = first + jnp.arange(count, dtype=jnp.int32)
    phase = modes[:, None] * index[None, :] % LON
    angle = phase.astype(jnp.float32) * (2.0 * math.pi / LON)
    factor = jnp.where(modes == 0, 1.0, 2.0).astype(jnp.float32)[:, None] / math.sqrt(LAT * LON)
    return jnp.stack([factor * jnp.cos(angle), -factor * jnp.sin(angle)]).astype(jnp.bfloat16)


def area_weights(first, count):
    index = first + jnp.arange(count, dtype=jnp.int32)
    return jnp.cos(math.pi * ((index.astype(jnp.float32) + 0.5) / LAT - 0.5))


def complex_block(pair):
    real_part, imag_part = (pair[0], pair[1])
    return jnp.stack(
        [jnp.stack([real_part, -imag_part], 1), jnp.stack([imag_part, real_part], 1)], 0
    )


def body(state, weights_in, bias_in, weights_out):
    batch, cdev, latdev, londev = state.shape
    nlat = lax.axis_size("lat")
    nlon = lax.axis_size("lon")
    lat_first = lax.axis_index("lat") * latdev
    lon_first = lax.axis_index("lon") * londev
    modes_lat = MLAT // nlat
    modes_lon = MLON // nlon
    qtab = lat_forward(lat_first, latdev)
    qsplit = qtab.reshape(2, 2, nlat, modes_lat, latdev)
    lonpart = jnp.einsum(
        "bcnl,lpk->pbcnk", state, lon_forward(lon_first, londev), preferred_element_type=jnp.float32
    )
    lonsplit = lonpart.reshape(2, batch, cdev, latdev, nlon, modes_lon)
    partial_value = jnp.einsum(
        "qpIJn,pbcnKk->qbcIKJk", qsplit, lonsplit, precision=lax.Precision.HIGHEST
    )
    spectrum = lax.psum_scatter(
        partial_value.reshape(2, batch, cdev, -1), ("lat", "lon"), scatter_dimension=3, tiled=True
    )
    spectrum = spectrum.astype(jnp.bfloat16)
    block_in = complex_block(weights_in)
    block_out = complex_block(weights_out)
    whole = lax.all_gather(spectrum, "var", axis=2, tiled=True)
    owned = lax.dynamic_slice_in_dim(block_out, lax.axis_index("var") * cdev, cdev, 1)
    hidden = jnp.einsum("qhpc,pbcj->qbhj", block_in, whole, preferred_element_type=jnp.float32)
    hidden = jnp.maximum(hidden + bias_in[:, None, :, None], 0.0).astype(jnp.bfloat16)
    mixed = jnp.einsum("qoph,pbhj->qboj", owned, hidden, preferred_element_type=jnp.float32).astype(
        jnp.bfloat16
    )
    mixed = mixed.reshape(2, batch, cdev, modes_lat, modes_lon)
    rtab = lat_inverse(lat_first, latdev)
    table = rtab
    latback = jnp.einsum(
        "qpnj,pbcjk->qbcnk",
        table,
        lax.all_gather(mixed, "lat", axis=3, tiled=True),
        preferred_element_type=jnp.float32,
    ).astype(jnp.bfloat16)
    htab = lon_inverse(lon_first, londev)
    table = htab
    result = jnp.einsum(
        "pbcnk,pkl->bcnl",
        lax.all_gather(latback, "lon", axis=4, tiled=True),
        table,
        preferred_element_type=jnp.float32,
    )
    active = jax.nn.gelu(result, approximate=False)
    field = active.astype(jnp.bfloat16)
    weights = area_weights(lat_first, latdev)
    denominator = batch * LON * jnp.sum(area_weights(0, LAT))
    row_total = jnp.sum(active, -1)
    row_square = jnp.sum(active * active, -1)
    summed, squared = lax.psum((row_total, row_square), "lon")
    zonal = summed / LON
    local = jnp.sum(squared * weights[None, None, :], axis=(0, 2))
    energy = lax.psum(local, "lat") / denominator
    return (field, zonal, energy)


def solution(mesh):
    return jax.shard_map(
        body,
        mesh=mesh,
        in_specs=(P(None, "var", "lat", "lon"), P(), P(), P()),
        out_specs=(P(None, "var", "lat", "lon"), P(None, "var", "lat"), P("var")),
        check_vma=False,
    )
```

profile of v0, /device:TPU:0, one launch (start us, length us, event | category | flops | bytes accessed | tf_op | source)
XLA Modules:
  0.0 286.0 jit_solution(11124718657220605227)
XLA Ops:
  7.2 0.0 reduce-scatter.2.cloned.1.call-start
  7.2 0.8 fusion.71
  8.1 0.3 fusion.82
  8.3 4.4 %fusion.15 = f32[2,96,64,96]{3,1,2,0:T(8,128)S(1)} fusion(bf16[1,64,96,512]{3,2,1,0:T(8,128)(2,1)} %param.4, f32[512,1,96]{0,2,1:T(8,128)S(1)} %get-tuple-element.24, f32[512,1,96]{0,2,1:T(8,128)S(1)} %get-tuple-element.23), kind=kOutput, calls=%fused_computation.25 | convolution fusion | flops 1208254464 | bytes 11403264 | tf_op jit(solution)/shard_map/bcnl,lpk->pbcnk/dot_general | solution.py:71
  12.8 12.8 %fusion.17 = f32[2,1,64,4,2,24,48]{2,5,3,0,6,4,1:T(8,128)} fusion(f32[2,64,96,2,48,1,1]{2,4,3,1,0,6,5:T(8,128)S(1)} %bitcast.169, f32[1,1,4,24,96]{4,3,1,2,0:T(8,128)S(1)} %get-tuple-element.20, f32[1,1,4,24,96]{4,3,1,2,0:T(8,128)S(1)} %get-tuple-element.19, f32[1,1,4,24,96]{4,3,1,2,0:T(8,128)S(1)} %get-tuple-element.18), kind=kOutput, calls=%fused_computation.28 | convolution fusion | flops 2718019584 | bytes 9547776 | tf_op jit(solution)/shard_map/qpIJn,pbcnKk->qbcIKJk/dot_general | solution.py:75
  25.6 12.4 %copy.27 = f32[2,1,64,4,2,24,48]{6,5,4,3,2,0,1:T(8,128)} copy(f32[2,1,64,4,2,24,48]{2,5,3,0,6,4,1:T(8,128)} %fusion.17) | data formatting | bytes 9437184 | tf_op jit(solution)/shard_map/qpIJn,pbcnKk->qbcIKJk/transpose | solution.py:75
  38.0 0.0 copy-start
  38.0 0.0 copy-start.1
  38.0 0.0 copy-start.2
  38.0 13.1 %reshape.714 = f32[2,1,64,9216]{3,2,0,1:T(8,128)} reshape(f32[2,1,64,4,2,24,48]{6,5,4,3,2,0,1:T(8,128)} %copy.27) | data formatting | bytes 9437184 | tf_op jit(solution)/shard_map/reshape | solution.py:79
  51.1 0.0 reduce-scatter.2.cloned.1.call-update
  51.1 0.0 all-gather.4.cloned.1.call-start
  51.2 56.6 %reduce-scatter.2.cloned.1.call-done = f32[2,1,64,1152]{3,2,0,1:T(8,128)} async-done(((f32[2,1,64,9216]{3,2,0,1:T(8,128)}), f32[2,1,64,1152]{3,2,0,1:T(8,128)}) %reduce-scatter.2.cloned.1.call-update) | async-done | bytes 589840 | tf_op jit(solution)/shard_map/reduce_scatter | solution.py:78
  107.8 1.1 convert_element_type.119
  108.9 1.0 copy.28
  109.9 0.0 all-gather.4.cloned.1.call-update
  109.9 0.2 all-gather.6.cloned.1.call-start
  110.2 0.0 copy-done
  110.2 0.0 copy-done.1
  110.3 0.1 maximum_bitcast_fusion
  110.4 30.0 %all-gather.4.cloned.1.call-done = bf16[2,1,256,1152]{3,0,1,2:T(2,128)(2,1)} async-done(((bf16[2,1,64,1152]{3,0,1,2:T(2,128)(2,1)}), bf16[2,1,256,1152]{3,0,1,2:T(2,128)(2,1)}) %all-gather.4.cloned.1.call-update) | async-done | bytes 1179664 | tf_op jit(solution)/shard_map/all_gather | solution.py:84
  140.3 3.5 %copy.29 = bf16[2,1,256,1152]{2,3,0,1:T(8,128)(2,1)S(1)} copy(bf16[2,1,256,1152]{3,0,1,2:T(2,128)(2,1)} %all-gather.4.cloned.1.call-done) | data formatting | bytes 2359296 | tf_op jit(solution)/shard_map/all_gather | solution.py:84
  143.8 0.0 copy-done.2
  143.8 1.1 fusion.28
  144.9 0.7 reshape.717
  145.7 1.3 copy.31
  147.0 0.0 all-gather.6.cloned.1.call-update
  147.0 0.0 all-gather.8.cloned.1.call-start
  147.1 0.3 negate_convert_fusion
  147.4 23.0 %all-gather.6.cloned.1.call-done = bf16[2,1,64,96,48]{2,4,1,0,3:T(8,128)(2,1)} async-done(((bf16[2,1,64,24,48]{2,4,1,0,3:T(8,128)(2,1)}), bf16[2,1,64,96,48]{2,4,1,0,3:T(8,128)(2,1)}) %all-gather.6.cloned.1.call-update) | async-done | bytes 1179664 | tf_op jit(solution)/shard_map/all_gather | solution.py:97
  170.4 4.4 %fusion.31 = bf16[2,1,64,96,48]{3,2,1,0,4:T(8,128)(2,1)} fusion(bf16[2,64,96,48,1]{1,3,0,2,4:T(8,128)(2,1)} %bitcast.170, bf16[1,2,96,96]{3,2,1,0:T(8,128)(2,1)S(1)} %get-tuple-element.17, bf16[1,2,96,96]{3,2,1,0:T(8,128)(2,1)S(1)} %get-tuple-element.16), kind=kOutput, calls=%fused_computation.41 | convolution fusion | flops 227229696 | bytes 2433024 | tf_op jit(solution)/shard_map/qpnj,pbcjk->qbcnk/dot_general | solution.py:94
  174.8 0.0 all-gather.8.cloned.1.call-update
  174.9 0.6 cosine_reduce_fusion
  176.2 0.1 multiply_cosine_fusion
  176.2 0.8 multiply_convert_fusion.1
  177.0 42.9 %all-gather.8.cloned.1.call-done = bf16[2,1,64,96,96]{3,2,1,0,4:T(8,128)(2,1)} async-done(((bf16[2,1,64,96,48]{3,2,1,0,4:T(8,128)(2,1)}), bf16[2,1,64,96,96]{3,2,1,0,4:T(8,128)(2,1)}) %all-gather.8.cloned.1.call-update) | async-done | bytes 2359312 | tf_op jit(solution)/shard_map/all_gather | solution.py:104
  219.9 4.8 %copy.34 = bf16[2,1,64,96,96]{4,3,0,2,1:T(8,128)(2,1)S(1)} copy(bf16[2,1,64,96,96]{3,2,1,0,4:T(8,128)(2,1)} %all-gather.8.cloned.1.call-done) | data formatting | bytes 4718592 | tf_op jit(solution)/shard_map/all_gather | solution.py:104
  224.7 40.1 %multiply_reduce_fusion = (f32[64,96]{1,0:T(8,128)S(1)}, f32[64,96]{1,0:T(8,128)S(1)}, bf16[1,64,96,512]{3,2,1,0:T(8,128)(2,1)}) fusion(bf16[1,96,512]{2,1,0:T(8,128)(2,1)S(1)} %get-tuple-element.22, bf16[1,96,512]{2,1,0:T(8,128)(2,1)S(1)} %get-tuple-element.21, bf16[2,1,64,96,96]{4,3,0,2,1:T(8,128)(2,1)S(1)} %copy.34), kind=kOutput, calls=%fused_computation.6 | convolution fusion | flops 1421955072 | bytes 8896512 | tf_op jit(solution)/shard_map/pbcnk,pkl->bcnl/dot_general | solution.py:102
  264.9 7.7 %all-reduce = (f32[1,64,96]{2,1,0:T(8,128)S(1)}, f32[1,64,96]{2,1,0:T(8,128)S(1)}) all-reduce(f32[1,64,96]{2,1,0:T(8,128)S(1)} %bitcast.172, f32[1,64,96]{2,1,0:T(8,128)S(1)} %bitcast.171), channel_id=1, replica_groups=mesh['var'=4,'lat'=4,'lon'=2] {'lon'}, use_global_device_ids=true, to_apply=%region_2.3 | all-reduce | flops 12288 | bytes 98304 | tf_op jit(solution)/shard_map/psum | solution.py:114
  272.5 0.6 broadcast_multiply_fusion
  273.2 0.1 multiply_reduce_fusion.1
  273.3 5.7 %psum.23 = f32[64]{0:T(128)S(1)} all-reduce(f32[64]{0:T(128)S(1)} %multiply_reduce_fusion.1), channel_id=1, replica_groups=mesh['var'=4,'lat'=4,'lon'=2] {'lat'}, use_global_device_ids=true, to_apply=%region_6.7 | all-reduce | flops 64 | bytes 512 | tf_op jit(solution)/shard_map/psum | solution.py:117
  278.9 0.5 broadcast_divide_fusion
  (9 shorter events, 0.1 us)
Async XLA Ops:
  7.2 100.6 %reduce-scatter.2.cloned.1.call-start = ((), (), s32[]{:S(2)}) async-start(), calls=%async_computation.1 | async-start | bytes 5308416 | tf_op jit(solution)/shard_map/reduce_scatter | solution.py:78
  38.0 72.2 %copy-start = (bf16[2,256,256]{2,1,0:T(8,128)(2,1)S(1)}, bf16[2,256,256]{2,1,0:T(8,128)(2,1)}, u32[]{:S(2)}) copy-start(bf16[2,256,256]{2,1,0:T(8,128)(2,1)} %param.5) | copy-start | bytes 786436
  38.0 72.2 %copy-start.1 = (bf16[2,256,256]{2,1,0:T(8,128)(2,1)S(1)}, bf16[2,256,256]{2,1,0:T(8,128)(2,1)}, u32[]{:S(2)}) copy-start(bf16[2,256,256]{2,1,0:T(8,128)(2,1)} %param.7) | copy-start | bytes 786436
  38.0 105.8 %copy-start.2 = (f32[2,256]{1,0:T(2,128)S(1)}, f32[2,256]{1,0:T(2,128)}, u32[]{:S(2)}) copy-start(f32[2,256]{1,0:T(2,128)} %param.6) | copy-start | bytes 6148
  51.1 89.2 %all-gather.4.cloned.1.call-start = ((), (), s32[]{:S(2)}) async-start(), calls=%async_computation.2 | async-start | bytes 1474560 | tf_op jit(solution)/shard_map/all_gather | solution.py:84
  109.9 60.5 %all-gather.6.cloned.1.call-start = ((), (), s32[]{:S(2)}) async-start(), calls=%async_computation.3 | async-start | bytes 2949120 | tf_op jit(solution)/shard_map/all_gather | solution.py:97
  147.0 72.9 %all-gather.8.cloned.1.call-start = ((), (), s32[]{:S(2)}) async-start(), calls=%async_computation.4 | async-start | bytes 4718592 | tf_op jit(solution)/shard_map/all_gather | solution.py:104
Sparse Core Ops, SparseCore 0:
  51.2 56.4 reduce-scatter.1
  110.0 30.2 all-gather.3
  147.1 23.2 all-gather.5
  175.0 44.9 all-gather.7
where the time goes:
time: 287 us; the launch traced here: 286 us
  waiting for transfers between devices  153 us (53%)
  matrix products  62.9 us (22%)
  local copies, waits for them, and re-layouts  36.8 us (13%)
  between operations  14.6 us (5%)
  blocking collectives  13.3 us (5%)
  other arithmetic  5.38 us (2%)
    reduce_scatter x1, waiting for transfers between devices, body(): lax.psum_scatter(partial_value.reshape(2, batch, cdev, -1), ('lat', 'lon'...  56.6 us
    all_gather x1, waiting for transfers between devices, body(): lax.all_gather(latback, 'lon', axis=4, tiled=True)  42.9 us
    dot_general x1, matrix products, body(): jnp.einsum('pbcnk,pkl->bcnl', lax.all_gather(latback, 'lon', axis=4, tile...  40.1 us
    all_gather x1, waiting for transfers between devices, body(): whole = lax.all_gather(spectrum, 'var', axis=2, tiled=True)  30 us
    all_gather x1, waiting for transfers between devices, body(): lax.all_gather(mixed, 'lat', axis=3, tiled=True)  23 us
    reshape x1, local copies, waits for them, and re-layouts, body(): partial_value.reshape(2, batch, cdev, -1)  13.1 us
    dot_general x1, matrix products, body(): jnp.einsum('qpIJn,pbcnKk->qbcIKJk', qsplit, lonsplit, precision=lax.Preci...  12.8 us
    transpose x1, local copies, waits for them, and re-layouts, body(): jnp.einsum('qpIJn,pbcnKk->qbcIKJk', qsplit, lonsplit, precision=lax.Preci...  12.4 us
  transfers between devices with their start and end apart: 4, of which 4 were waited for; matrix products, arithmetic and copies ran while one was open for 1% of the time, Pallas kernels for 0%

commit v1 on v0

--- a/solution.py
+++ b/solution.py
@@ -81,7 +81,12 @@
     spectrum = spectrum.astype(jnp.bfloat16)
     block_in = complex_block(weights_in)
     block_out = complex_block(weights_out)
-    whole = lax.all_gather(spectrum, "var", axis=2, tiled=True)
+    ring = [spectrum]
+    for hop in range(3):
+        ring.append(lax.ppermute(ring[-1], "var", [(dev, (dev + 1) % 4) for dev in range(4)]))
+    whole = jnp.roll(
+        jnp.concatenate(ring[::-1], axis=2), (lax.axis_index("var") + 1) * ring[0].shape[2], axis=2
+    )
     owned = lax.dynamic_slice_in_dim(block_out, lax.axis_index("var") * cdev, cdev, 1)
     hidden = jnp.einsum("qhpc,pbcj->qbhj", block_in, whole, preferred_element_type=jnp.float32)
     hidden = jnp.maximum(hidden + bias_in[:, None, :, None], 0.0).astype(jnp.bfloat16)

time: 287 us -> 284 us (0.990)
  waiting for transfers between devices: 153 us -> 147 us
  local copies, waits for them, and re-layouts: 36.8 us -> 33.9 us
    all_gather x1 -> x0, waiting for transfers between devices: 30 us -> none  [body(): whole = lax.all_gather(spectrum, 'var', axis=2, tiled=True)]
    ppermute x0 -> x3, waiting for transfers between devices: none -> 26.9 us  [body(): lax.ppermute(ring[-1], 'var', [(dev, (dev + 1) % 4) for dev in range(4)])]
    all_gather x1 -> x0, local copies, waits for them, and re-layouts: 3.45 us -> none  [body(): whole = lax.all_gather(spectrum, 'var', axis=2, tiled=True)]
  transfers between devices with their start and end apart: 4 -> 6, of which waited for: 4 -> 6; matrix products, arithmetic and copies ran while one was open for 1% -> 1% of each run, Pallas kernels for 0% -> 0%
where the time goes in v1:
time: 284 us; the launch traced here: 283 us
  waiting for transfers between devices  147 us (52%)
  matrix products  64.2 us (23%)
  local copies, waits for them, and re-layouts  33.9 us (12%)
  between operations  14.6 us (5%)
  blocking collectives  13.3 us (5%)
  other arithmetic  7.59 us (3%)
    reduce_scatter x1, waiting for transfers between devices, body(): lax.psum_scatter(partial_value.reshape(2, batch, cdev, -1), ('lat', 'lon'...  56.6 us
    all_gather x1, waiting for transfers between devices, body(): lax.all_gather(latback, 'lon', axis=4, tiled=True)  42.9 us
    dot_general x1, matrix products, body(): jnp.einsum('pbcnk,pkl->bcnl', lax.all_gather(latback, 'lon', axis=4, tile...  40.1 us
    ppermute x3, waiting for transfers between devices, body(): lax.ppermute(ring[-1], 'var', [(dev, (dev + 1) % 4) for dev in range(4)])  26.9 us
    all_gather x1, waiting for transfers between devices, body(): lax.all_gather(mixed, 'lat', axis=3, tiled=True)  21 us
    reshape x1, local copies, waits for them, and re-layouts, body(): partial_value.reshape(2, batch, cdev, -1)  13.1 us
    dot_general x1, matrix products, body(): jnp.einsum('qpIJn,pbcnKk->qbcIKJk', qsplit, lonsplit, precision=lax.Preci...  12.8 us
    transpose x1, local copies, waits for them, and re-layouts, body(): jnp.einsum('qpIJn,pbcnKk->qbcIKJk', qsplit, lonsplit, precision=lax.Preci...  12.3 us
  transfers between devices with their start and end apart: 6, of which 6 were waited for; matrix products, arithmetic and copies ran while one was open for 1% of the time, Pallas kernels for 0%

profile of v1, /device:TPU:0, one launch (start us, length us, event | category | flops | bytes accessed | tf_op | source)
XLA Modules:
  0.0 282.8 jit_solution(7830496611080861767)
XLA Ops:
  7.2 0.0 reduce-scatter.2.cloned.1.call-start
  7.2 0.8 fusion.72
  8.1 0.3 fusion.83
  8.3 4.4 %fusion.15 = f32[2,96,64,96]{3,1,2,0:T(8,128)S(1)} fusion(bf16[1,64,96,512]{3,2,1,0:T(8,128)(2,1)} %param.4, f32[512,1,96]{0,2,1:T(8,128)S(1)} %get-tuple-element.24, f32[512,1,96]{0,2,1:T(8,128)S(1)} %get-tuple-element.23), kind=kOutput, calls=%fused_computation.25 | convolution fusion | flops 1208254464 | bytes 11403264 | tf_op jit(solution)/shard_map/bcnl,lpk->pbcnk/dot_general | solution.py:71
  12.8 12.8 %fusion.17 = f32[2,1,64,4,2,24,48]{2,5,3,0,6,4,1:T(8,128)} fusion(f32[2,64,96,2,48,1,1]{2,4,3,1,0,6,5:T(8,128)S(1)} %bitcast.170, f32[1,1,4,24,96]{4,3,1,2,0:T(8,128)S(1)} %get-tuple-element.20, f32[1,1,4,24,96]{4,3,1,2,0:T(8,128)S(1)} %get-tuple-element.19, f32[1,1,4,24,96]{4,3,1,2,0:T(8,128)S(1)} %get-tuple-element.18), kind=kOutput, calls=%fused_computation.28 | convolution fusion | flops 2718019584 | bytes 9547776 | tf_op jit(solution)/shard_map/qpIJn,pbcnKk->qbcIKJk/dot_general | solution.py:75
  25.6 12.3 %copy.26 = f32[2,1,64,4,2,24,48]{6,5,4,3,2,0,1:T(8,128)} copy(f32[2,1,64,4,2,24,48]{2,5,3,0,6,4,1:T(8,128)} %fusion.17) | data formatting | bytes 9437184 | tf_op jit(solution)/shard_map/qpIJn,pbcnKk->qbcIKJk/transpose | solution.py:75
  37.9 0.0 copy-start
  38.0 0.0 copy-start.1
  38.0 0.0 copy-start.3
  38.0 13.1 %reshape.714 = f32[2,1,64,9216]{3,2,0,1:T(8,128)} reshape(f32[2,1,64,4,2,24,48]{6,5,4,3,2,0,1:T(8,128)} %copy.26) | data formatting | bytes 9437184 | tf_op jit(solution)/shard_map/reshape | solution.py:79
  51.1 0.0 reduce-scatter.2.cloned.1.call-update
  51.1 0.0 all-gather.3.cloned.1.call-start
  51.2 56.6 %reduce-scatter.2.cloned.1.call-done = f32[2,1,64,1152]{3,2,0,1:T(8,128)} async-done(((f32[2,1,64,9216]{3,2,0,1:T(8,128)}), f32[2,1,64,1152]{3,2,0,1:T(8,128)}) %reduce-scatter.2.cloned.1.call-update) | async-done | bytes 589840 | tf_op jit(solution)/shard_map/reduce_scatter | solution.py:78
  107.7 1.1 convert_element_type.119
  108.8 1.5 collective-permute-start
  110.4 0.0 copy-done
  110.4 8.9 %collective-permute-done = bf16[2,1,64,1152]{3,2,0,1:T(8,128)(2,1)S(1)} collective-permute-done((bf16[2,1,64,1152]{3,2,0,1:T(8,128)(2,1)S(1)}, bf16[2,1,64,1152]{3,2,0,1:T(8,128)(2,1)S(1)}, u32[]{:S(2)}, u32[]{:S(2)}) %collective-permute-start) | collective-permute-done | bytes 294944 | tf_op jit(solution)/shard_map/ppermute | solution.py:86
  119.3 0.0 collective-permute-start.1
  119.3 0.0 copy-done.1
  119.4 9.5 %collective-permute-done.1 = bf16[2,1,64,1152]{3,2,0,1:T(8,128)(2,1)S(1)} collective-permute-done((bf16[2,1,64,1152]{3,2,0,1:T(8,128)(2,1)S(1)}, bf16[2,1,64,1152]{3,2,0,1:T(8,128)(2,1)S(1)}, u32[]{:S(2)}, u32[]{:S(2)}) %collective-permute-start.1) | collective-permute-done | bytes 294944 | tf_op jit(solution)/shard_map/ppermute | solution.py:86
  128.8 0.0 collective-permute-start.2
  128.9 0.1 maximum_bitcast_fusion
  129.0 8.6 %collective-permute-done.2 = bf16[2,1,64,1152]{3,2,0,1:T(8,128)(2,1)S(1)} collective-permute-done((bf16[2,1,64,1152]{3,2,0,1:T(8,128)(2,1)S(1)}, bf16[2,1,64,1152]{3,2,0,1:T(8,128)(2,1)S(1)}, u32[]{:S(2)}, u32[]{:S(2)}) %collective-permute-start.2) | collective-permute-done | bytes 294944 | tf_op jit(solution)/shard_map/ppermute | solution.py:86
  137.6 1.1 constant_dynamic-update-slice_fusion.4
  138.8 1.1 constant_dynamic-update-slice_fusion
  140.0 0.0 copy-start.2
  140.0 1.4 copy-done.2
  141.4 0.0 copy-done.3
  141.4 2.4 fusion.28
  143.8 0.7 reshape.717
  144.5 1.3 copy.29
  145.8 0.0 all-gather.3.cloned.1.call-update
  145.9 0.0 all-gather.5.cloned.1.call-start
  145.9 0.3 negate_convert_fusion
  146.2 21.0 %all-gather.3.cloned.1.call-done = bf16[2,1,64,96,48]{2,4,1,0,3:T(8,128)(2,1)} async-done(((bf16[2,1,64,24,48]{2,4,1,0,3:T(8,128)(2,1)}), bf16[2,1,64,96,48]{2,4,1,0,3:T(8,128)(2,1)}) %all-gather.3.cloned.1.call-update) | async-done | bytes 1179664 | tf_op jit(solution)/shard_map/all_gather | solution.py:102
  167.3 4.4 %fusion.31 = bf16[2,1,64,96,48]{3,2,1,0,4:T(8,128)(2,1)} fusion(bf16[2,64,96,48,1]{1,3,0,2,4:T(8,128)(2,1)} %bitcast.171, bf16[1,2,96,96]{3,2,1,0:T(8,128)(2,1)S(1)} %get-tuple-element.17, bf16[1,2,96,96]{3,2,1,0:T(8,128)(2,1)S(1)} %get-tuple-element.16), kind=kOutput, calls=%fused_computation.41 | convolution fusion | flops 227229696 | bytes 2433024 | tf_op jit(solution)/shard_map/qpnj,pbcjk->qbcnk/dot_general | solution.py:99
  171.6 0.0 all-gather.5.cloned.1.call-update
  171.7 0.6 cosine_reduce_fusion
  173.0 0.1 multiply_cosine_fusion
  173.0 0.8 multiply_convert_fusion.1
  173.9 42.9 %all-gather.5.cloned.1.call-done = bf16[2,1,64,96,96]{3,2,1,0,4:T(8,128)(2,1)} async-done(((bf16[2,1,64,96,48]{3,2,1,0,4:T(8,128)(2,1)}), bf16[2,1,64,96,96]{3,2,1,0,4:T(8,128)(2,1)}) %all-gather.5.cloned.1.call-update) | async-done | bytes 2359312 | tf_op jit(solution)/shard_map/all_gather | solution.py:109
  216.7 4.8 %copy.32 = bf16[2,1,64,96,96]{4,3,0,2,1:T(8,128)(2,1)S(1)} copy(bf16[2,1,64,96,96]{3,2,1,0,4:T(8,128)(2,1)} %all-gather.5.cloned.1.call-done) | data formatting | bytes 4718592 | tf_op jit(solution)/shard_map/all_gather | solution.py:109
  221.5 40.1 %multiply_reduce_fusion = (f32[64,96]{1,0:T(8,128)S(1)}, f32[64,96]{1,0:T(8,128)S(1)}, bf16[1,64,96,512]{3,2,1,0:T(8,128)(2,1)}) fusion(bf16[1,96,512]{2,1,0:T(8,128)(2,1)S(1)} %get-tuple-element.22, bf16[1,96,512]{2,1,0:T(8,128)(2,1)S(1)} %get-tuple-element.21, bf16[2,1,64,96,96]{4,3,0,2,1:T(8,128)(2,1)S(1)} %copy.32), kind=kOutput, calls=%fused_computation.6 | convolution fusion | flops 1421955072 | bytes 8896512 | tf_op jit(solution)/shard_map/pbcnk,pkl->bcnl/dot_general | solution.py:107
  261.7 7.7 %all-reduce = (f32[1,64,96]{2,1,0:T(8,128)S(1)}, f32[1,64,96]{2,1,0:T(8,128)S(1)}) all-reduce(f32[1,64,96]{2,1,0:T(8,128)S(1)} %bitcast.173, f32[1,64,96]{2,1,0:T(8,128)S(1)} %bitcast.172), channel_id=1, replica_groups=mesh['var'=4,'lat'=4,'lon'=2] {'lon'}, use_global_device_ids=true, to_apply=%region_2.3 | all-reduce | flops 12288 | bytes 98304 | tf_op jit(solution)/shard_map/psum | solution.py:119
  269.4 0.6 broadcast_multiply_fusion
  270.0 0.1 multiply_reduce_fusion.1
  270.1 5.7 %psum.23 = f32[64]{0:T(128)S(1)} all-reduce(f32[64]{0:T(128)S(1)} %multiply_reduce_fusion.1), channel_id=1, replica_groups=mesh['var'=4,'lat'=4,'lon'=2] {'lat'}, use_global_device_ids=true, to_apply=%region_6.7 | all-reduce | flops 64 | bytes 512 | tf_op jit(solution)/shard_map/psum | solution.py:122
  275.7 0.5 broadcast_divide_fusion
  (15 shorter events, 0.3 us)
Async XLA Ops:
  7.2 100.6 %reduce-scatter.2.cloned.1.call-start = ((), (), s32[]{:S(2)}) async-start(), calls=%async_computation.1 | async-start | bytes 5308416 | tf_op jit(solution)/shard_map/reduce_scatter | solution.py:78
  37.9 72.4 %copy-start = (bf16[2,256,256]{2,1,0:T(8,128)(2,1)S(1)}, bf16[2,256,256]{2,1,0:T(8,128)(2,1)}, u32[]{:S(2)}) copy-start(bf16[2,256,256]{2,1,0:T(8,128)(2,1)} %param.5) | copy-start | bytes 786436
  38.0 81.4 %copy-start.1 = (bf16[2,256,256]{2,1,0:T(8,128)(2,1)S(1)}, bf16[2,256,256]{2,1,0:T(8,128)(2,1)}, u32[]{:S(2)}) copy-start(bf16[2,256,256]{2,1,0:T(8,128)(2,1)} %param.7) | copy-start | bytes 786436
  38.0 103.4 %copy-start.3 = (f32[2,256]{1,0:T(2,128)S(1)}, f32[2,256]{1,0:T(2,128)}, u32[]{:S(2)}) copy-start(f32[2,256]{1,0:T(2,128)} %param.6) | copy-start | bytes 6148
  51.1 116.2 %all-gather.3.cloned.1.call-start = ((), (), s32[]{:S(2)}) async-start(), calls=%async_computation.2 | async-start | bytes 2949120 | tf_op jit(solution)/shard_map/all_gather | solution.py:102
  108.8 10.4 %collective-permute-start = (bf16[2,1,64,1152]{3,2,0,1:T(8,128)(2,1)S(1)}, bf16[2,1,64,1152]{3,2,0,1:T(8,128)(2,1)S(1)}, u32[]{:S(2)}, u32[]{:S(2)}) collective-permute-start(bf16[2,1,64,1152]{3,2,0,1:T(8,128)(2,1)S(1)} %convert_element_type.119), channel_id=1, source_target_pairs={{0,8},{8,16},{16,24},{24,0},{1,9},{9,17},{17,25},{25,1},{2,10},{10... | collective-permute-start | bytes 884744 | tf_op jit(solution)/shard_map/ppermute | solution.py:86
  119.3 9.5 %collective-permute-start.1 = (bf16[2,1,64,1152]{3,2,0,1:T(8,128)(2,1)S(1)}, bf16[2,1,64,1152]{3,2,0,1:T(8,128)(2,1)S(1)}, u32[]{:S(2)}, u32[]{:S(2)}) collective-permute-start(bf16[2,1,64,1152]{3,2,0,1:T(8,128)(2,1)S(1)} %collective-permute-done), channel_id=1, source_target_pairs={{0,8},{8,16},{16,24},{24,0},{1,9},{9,17},{17,25},{25,1},{2,10},{10... | collective-permute-start | bytes 884744 | tf_op jit(solution)/shard_map/ppermute | solution.py:86
  128.8 8.7 %collective-permute-start.2 = (bf16[2,1,64,1152]{3,2,0,1:T(8,128)(2,1)S(1)}, bf16[2,1,64,1152]{3,2,0,1:T(8,128)(2,1)S(1)}, u32[]{:S(2)}, u32[]{:S(2)}) collective-permute-start(bf16[2,1,64,1152]{3,2,0,1:T(8,128)(2,1)S(1)} %collective-permute-done.1), channel_id=1, source_target_pairs={{0,8},{8,16},{16,24},{24,0},{1,9},{9,17},{17,25},{25,1},{2,10},{10... | collective-permute-start | bytes 884744 | tf_op jit(solution)/shard_map/ppermute | solution.py:86
  140.0 1.4 copy-start.2
  145.9 70.9 %all-gather.5.cloned.1.call-start = ((), (), s32[]{:S(2)}) async-start(), calls=%async_computation.3 | async-start | bytes 4718592 | tf_op jit(solution)/shard_map/all_gather | solution.py:109
Sparse Core Ops, SparseCore 0:
  51.2 56.4 reduce-scatter.1
  146.0 21.2 all-gather.2
  171.8 44.9 all-gather.4
